TPU v7x, 32 devices: a whole 2x2x4 slice. The times are simulated.
32 devices in a mesh: cube: 2 (over y), gz: 8 (over z, x), gy: 2 (over core).
Axes of the slice: x: 2, y: 2, z: 4, core: 2. Of those that a mesh axis runs over, the one named last changes fastest.
Arguments:
- noisy_cube: float32 [64, 64, 256], P(('cube', 'gz'), 'gy'), parts along dimension 0, may hold values from -40 to 40
- thresholds: float32 [4], replicated, may hold values from 0.5 to 4
Outputs:
- denoised: float32 [64, 4, 64, 256], P(('cube', 'gz'), None, 'gy'), parts along dimension 0
- gcv_score: float32 [8], P('cube'), parts along dimension 0
There are 2 independent parts, one for each index of `cube`. A program takes and returns all parts, laid end to end along the dimension named above; an argument that names none is the same for every part. Nothing has to cross between parts.
All inputs are finite; a program needn't handle non-finite values.
Results may differ from a plain program's by a relative error of at most 0.0003.
Values sent between devices are 32-bit elements; how exact they have to be, the bound alone decides.
No kernel may reach another device: no remote copies, remote signals or barrier semaphores. Data moves between devices by JAX's collectives and lax.ppermute only.
A program may use at most 64 MiB of HBM per device.

v0:
```python
import jax
import jax.numpy as jnp
from jax import lax
from jax.sharding import PartitionSpec as P

LOWPASS = (
    0.2303778133088964,
    0.7148465705529155,
    0.6308807679298587,
    -0.0279837694168599,
    -0.1870348117190931,
    0.0308413818355607,
    0.0328830116668852,
    -0.010597401785069,
)
HIGHPASS = tuple(((-1) ** tap_index * LOWPASS[7 - tap_index] for tap_index in range(8)))
lead_taps = 6
trail_taps = 3


def passed_along(array, axis, by):
    devices = lax.axis_size(axis)
    return lax.ppermute(array, axis, [(i, (i + by) % devices) for i in range(devices)])


def analyse(extended, dimension_number, axis_length):
    lowband = 0.0
    highband = 0.0
    for tap_index in range(8):
        sliced = lax.slice_in_dim(
            extended, tap_index, tap_index + axis_length - 1, 2, dimension_number
        )
        lowband = lowband + LOWPASS[tap_index] * sliced
        highband = highband + HIGHPASS[tap_index] * sliced
    return (lowband, highband)


def synthesise(lowband, highband, dimension_number, axis_length):
    even_part = 0.0
    odd_part = 0.0
    for tap_index in range(4):
        low_slice = lax.slice_in_dim(
            lowband, 3 - tap_index, 3 - tap_index + axis_length, 1, dimension_number
        )
        high_slice = lax.slice_in_dim(
            highband, 3 - tap_index, 3 - tap_index + axis_length, 1, dimension_number
        )
        even_part = (
            even_part + LOWPASS[2 * tap_index] * low_slice + HIGHPASS[2 * tap_index] * high_slice
        )
        odd_part = (
            odd_part
            + LOWPASS[2 * tap_index + 1] * low_slice
            + HIGHPASS[2 * tap_index + 1] * high_slice
        )
    paired = jnp.stack([even_part, odd_part], dimension_number + 1)
    target = list(even_part.shape)
    target[dimension_number] = 2 * axis_length
    return paired.reshape(target)


def merge_bands(lowband, highband):
    stacked = jnp.stack([lowband, highband], 2)
    return stacked.reshape((lowband.shape[0], 2 * lowband.shape[1]) + lowband.shape[2:])


def split_bands(current):
    halves = current.reshape((current.shape[0], current.shape[1] // 2, 2) + current.shape[2:])
    return (halves[:, :, 0], halves[:, :, 1])


def wrap_ahead(input_tensor, dimension_number, border_extent):
    return jnp.concatenate(
        [input_tensor, lax.slice_in_dim(input_tensor, 0, border_extent, 1, dimension_number)],
        dimension_number,
    )


def wrap_behind(input_tensor, dimension_number, border_extent):
    axis_length = input_tensor.shape[dimension_number]
    return jnp.concatenate(
        [
            lax.slice_in_dim(
                input_tensor, axis_length - border_extent, axis_length, 1, dimension_number
            ),
            input_tensor,
        ],
        dimension_number,
    )


def z_shift(input_tensor, start_offset):
    return passed_along(input_tensor, "gz", start_offset)


def y_shift(input_tensor, start_offset):
    return passed_along(input_tensor, "gy", start_offset)


def following_panel(input_tensor, dimension_number, border_extent, holding_tensor):
    axis_length = input_tensor.shape[dimension_number]
    split_pieces = [input_tensor]
    covered = 0
    start_offset = 1
    while covered < border_extent:
        shift_amount = min(axis_length, border_extent - covered)
        split_pieces.append(
            holding_tensor(
                lax.slice_in_dim(input_tensor, 0, shift_amount, 1, dimension_number), -start_offset
            )
        )
        covered += shift_amount
        start_offset += 1
    return jnp.concatenate(split_pieces, dimension_number)


def preceding_panel(input_tensor, dimension_number, border_extent, holding_tensor):
    axis_length = input_tensor.shape[dimension_number]
    split_pieces = [input_tensor]
    covered = 0
    start_offset = 1
    while covered < border_extent:
        shift_amount = min(axis_length, border_extent - covered)
        split_pieces.insert(
            0,
            holding_tensor(
                lax.slice_in_dim(
                    input_tensor, axis_length - shift_amount, axis_length, 1, dimension_number
                ),
                start_offset,
            ),
        )
        covered += shift_amount
        start_offset += 1
    return jnp.concatenate(split_pieces, dimension_number)


def forward_level(volume):
    planes, number_of_lines, col_count = (volume.shape[0], volume.shape[2], volume.shape[3])
    lowband, highband = analyse(following_panel(volume, 0, lead_taps, z_shift), 0, planes)
    banded = merge_bands(lowband, highband)
    lowband, highband = analyse(following_panel(banded, 2, lead_taps, y_shift), 2, number_of_lines)
    banded = merge_bands(lowband, highband)
    lowband, highband = analyse(wrap_ahead(banded, 3, lead_taps), 3, col_count)
    return merge_bands(lowband, highband)


def synth_x(current):
    lowband, highband = split_bands(current)
    return synthesise(
        wrap_behind(lowband, 3, trail_taps),
        wrap_behind(highband, 3, trail_taps),
        3,
        current.shape[3],
    )


def synth_y(extended, number_of_lines):
    lowband, highband = split_bands(extended)
    return synthesise(lowband, highband, 2, number_of_lines)


def synth_z(extended, planes):
    lowband, highband = split_bands(extended)
    return synthesise(lowband, highband, 0, planes)


def inverse_level(coeffs):
    planes, number_of_lines = (coeffs.shape[0], coeffs.shape[2])
    current = synth_x(coeffs)
    current = synth_y(preceding_panel(current, 2, trail_taps, y_shift), number_of_lines)
    return synth_z(preceding_panel(current, 0, trail_taps, z_shift), planes)


def spread(details, approximation, limits):
    bounds = limits[None, :, None, None, None]
    widened = details[:, None]
    shrunk = widened - jnp.clip(widened, -bounds, bounds)
    complete = jnp.concatenate([approximation[:, :, None], shrunk], 2)
    return complete.reshape((complete.shape[0], complete.shape[1] * 8) + complete.shape[3:])


def body(noisy_cube, thresholds):
    planes, number_of_lines, col_count = noisy_cube.shape
    level_one = forward_level(noisy_cube[:, None])
    level_two = forward_level(level_one[:, :1])
    details_one = level_one[:, 1:]
    details_two = level_two[:, 1:]
    squares = thresholds * thresholds
    square_grid = squares[:, None, None, None, None]

    def weights(details):
        widened = details[None]
        return jnp.sum(square_grid / (square_grid + widened * widened), axis=(1, 2, 3, 4))

    zero_local = weights(details_one) + weights(details_two)
    zero_weight = lax.psum(zero_local, ("gz", "gy"))
    count_two = level_two.shape
    coarse_two = jnp.broadcast_to(
        level_two[:, :1], (count_two[0], thresholds.shape[0], count_two[2], count_two[3])
    )
    approximation = inverse_level(spread(details_two, coarse_two, thresholds))
    denoised = inverse_level(spread(details_one, approximation, thresholds))
    residual = lax.psum(
        jnp.sum((denoised - noisy_cube[:, None]) ** 2, axis=(0, 2, 3)), ("gz", "gy")
    )
    cell_count = planes * number_of_lines * col_count * lax.axis_size("gz") * lax.axis_size("gy")
    gcv_score = cell_count * residual / (zero_weight * zero_weight)
    return (denoised, gcv_score)


def solution(mesh):
    in_specs = (P(("cube", "gz"), "gy", None), P())
    out_specs = (P(("cube", "gz"), None, "gy", None), P("cube"))
    return jax.shard_map(body, mesh=mesh, in_specs=in_specs, out_specs=out_specs, check_vma=False)
```

profile of v0, /device:TPU:0, one launch (start us, length us, event | category | flops | bytes accessed | tf_op | source)
XLA Modules:
  0.0 137.7 jit_solution(2075834466004949712)
XLA Ops:
  0.6 6.1 %collective-permute-start = (f32[4,1,32,256]{3,2,0,1:T(8,128)}, f32[4,1,32,256]{3,2,0,1:T(8,128)S(1)}, u32[]{:S(2)}, u32[]{:S(2)}) collective-permute-start(f32[4,1,32,256]{3,2,0,1:T(8,128)} %bitcast.244), channel_id=1, source_target_pairs={{0,14},{2,0},{4,2},{6,4},{8,6},{10,8},{12,10},{14,12},{1,15},{3,1}... | collective-permute-start | bytes 393224 | tf_op jit(solution)/shard_map/ppermute | solution.py:23
  6.7 0.9 slice_bitcast_fusion.4
  7.6 0.4 collective-permute-start.1
  8.0 3.8 %collective-permute-done.1 = f32[2,1,32,256]{3,2,0,1:T(8,128)S(1)} collective-permute-done((f32[2,1,32,256]{3,2,0,1:T(8,128)S(1)}, f32[2,1,32,256]{3,2,0,1:T(8,128)S(1)}, u32[]{:S(2)}, u32[]{:S(2)}) %collective-permute-start.1) | collective-permute-done | bytes 65568 | tf_op jit(solution)/shard_map/ppermute | solution.py:23
  11.8 0.9 pad_maximum_fusion.5
  12.8 1.0 add_bitcast_fusion.11
  14.0 1.0 collective-permute-done.2
  15.8 2.3 %slice.438 = f32[2,4,16,128]{3,2,1,0:T(8,128)S(1)} slice(f32[2,4,16,256]{3,2,1,0:T(8,128)S(1)} %bitcast.249), slice={[0:2:1], [0:4:1], [0:16:1], [1:256:2]} | slice | bytes 131072 | tf_op jit(solution)/shard_map/slice | solution.py:30
  18.1 2.3 %slice.437 = f32[2,4,16,128]{3,2,1,0:T(8,128)S(1)} slice(f32[2,4,16,256]{3,2,1,0:T(8,128)S(1)} %bitcast.250), slice={[0:2:1], [0:4:1], [0:16:1], [0:255:2]} | slice | bytes 131072 | tf_op jit(solution)/shard_map/slice | solution.py:30
  20.5 2.3 %slice.445 = f32[2,4,16,128]{3,2,1,0:T(8,128)S(1)} slice(f32[2,4,16,262]{3,2,1,0:T(8,128)S(1)} %pad_maximum_fusion.9), slice={[0:2:1], [0:4:1], [0:16:1], [7:262:2]} | slice | bytes 131072 | tf_op jit(solution)/shard_map/slice | solution.py:30
  22.9 2.3 %slice.444 = f32[2,4,16,128]{3,2,1,0:T(8,128)S(1)} slice(f32[2,4,16,262]{3,2,1,0:T(8,128)S(1)} %pad_maximum_fusion.9), slice={[0:2:1], [0:4:1], [0:16:1], [6:261:2]} | slice | bytes 131072 | tf_op jit(solution)/shard_map/slice | solution.py:30
  25.2 2.3 %slice.443 = f32[2,4,16,128]{3,2,1,0:T(8,128)S(1)} slice(f32[2,4,16,262]{3,2,1,0:T(8,128)S(1)} %pad_maximum_fusion.9), slice={[0:2:1], [0:4:1], [0:16:1], [5:260:2]} | slice | bytes 131072 | tf_op jit(solution)/shard_map/slice | solution.py:30
  27.5 2.3 %slice.442 = f32[2,4,16,128]{3,2,1,0:T(8,128)S(1)} slice(f32[2,4,16,262]{3,2,1,0:T(8,128)S(1)} %pad_maximum_fusion.9), slice={[0:2:1], [0:4:1], [0:16:1], [4:259:2]} | slice | bytes 131072 | tf_op jit(solution)/shard_map/slice | solution.py:30
  29.9 2.3 %slice.441 = f32[2,4,16,128]{3,2,1,0:T(8,128)S(1)} slice(f32[2,4,16,262]{3,2,1,0:T(8,128)S(1)} %pad_maximum_fusion.9), slice={[0:2:1], [0:4:1], [0:16:1], [3:258:2]} | slice | bytes 131072 | tf_op jit(solution)/shard_map/slice | solution.py:30
  32.2 2.3 %slice.440 = f32[2,4,16,128]{3,2,1,0:T(8,128)S(1)} slice(f32[2,4,16,262]{3,2,1,0:T(8,128)S(1)} %pad_maximum_fusion.9), slice={[0:2:1], [0:4:1], [0:16:1], [2:257:2]} | slice | bytes 131072 | tf_op jit(solution)/shard_map/slice | solution.py:30
  34.7 0.9 collective-permute-start.5
  35.7 2.7 %collective-permute-start.4 = (f32[2,1,16,128]{3,2,1,0:T(8,128)S(1)}, f32[2,1,16,128]{3,2,1,0:T(8,128)S(1)}, u32[]{:S(2)}, u32[]{:S(2)}) collective-permute-start(f32[2,1,16,128]{3,2,1,0:T(8,128)S(1)} %slice.541), channel_id=1, source_target_pairs={{0,12},{2,14},{4,0},{6,2},{8,4},{10,6},{12,8},{14,10},{1,13},{3,15... | collective-permute-start | bytes 49160 | tf_op jit(solution)/shard_map/ppermute | solution.py:23
  38.6 0.8 collective-permute-done.5
  39.4 1.3 collective-permute-done.4
  40.7 1.3 collective-permute-done.3
  42.2 1.1 collective-permute-done.6
  44.2 0.3 slice.472
  44.5 0.3 slice.471
  44.9 0.3 slice.470
  45.2 0.3 slice.469
  45.5 0.3 slice.468
  45.9 0.3 slice.467
  46.6 0.4 add_bitcast_fusion.5
  47.6 0.6 copy.325
  48.5 0.5 collective-permute-done.7
  49.2 3.8 %collective-permute-start.10 = (f32[1,8,16,128]{3,1,2,0:T(8,128)S(1)}, f32[1,8,16,128]{3,1,2,0:T(8,128)S(1)}, u32[]{:S(2)}, u32[]{:S(2)}) collective-permute-start(f32[1,8,16,128]{3,1,2,0:T(8,128)S(1)} %bitcast.270), channel_id=1, source_target_pairs={{0,6},{2,8},{4,10},{6,12},{8,14},{10,0},{12,2},{14,4},{1,7},{3,9},... | collective-permute-start | bytes 196616 | tf_op jit(solution)/shard_map/ppermute | solution.py:23
  53.2 0.9 collective-permute-start.8
  54.1 2.6 %collective-permute-done.10 = f32[1,8,16,128]{3,1,2,0:T(8,128)S(1)} collective-permute-done((f32[1,8,16,128]{3,1,2,0:T(8,128)S(1)}, f32[1,8,16,128]{3,1,2,0:T(8,128)S(1)}, u32[]{:S(2)}, u32[]{:S(2)}) %collective-permute-start.10) | collective-permute-done | bytes 65568 | tf_op jit(solution)/shard_map/ppermute | solution.py:23
  56.8 2.5 %collective-permute-done.9 = f32[1,8,16,128]{3,1,2,0:T(8,128)S(1)} collective-permute-done((f32[1,8,16,128]{3,1,2,0:T(8,128)S(1)}, f32[1,8,16,128]{3,1,2,0:T(8,128)S(1)}, u32[]{:S(2)}, u32[]{:S(2)}) %collective-permute-start.9) | collective-permute-done | bytes 65568 | tf_op jit(solution)/shard_map/ppermute | solution.py:23
  59.3 1.1 collective-permute-done.8
  60.9 1.3 add_bitcast_fusion.3
  62.3 4.3 %copy.350 = f32[2,16,16,128,2]{2,1,4,3,0:T(8,128)} copy(f32[2,16,16,128,2]{3,2,1,0,4:T(8,128)S(1)} %pad_maximum_fusion.2) | data formatting | bytes 1048576 | tf_op jit(solution)/shard_map/stack | solution.py:56
  66.6 5.4 %slice.596 = f32[2,16,3,256]{2,1,3,0:T(8,128)} slice(f32[2,16,16,256]{2,1,3,0:T(8,128)} %bitcast.235), slice={[0:2], [0:16], [13:16], [0:256]} | slice | bytes 196608 | tf_op jit(solution)/shard_map/slice | solution.py:127
  72.0 3.5 %copy.351 = f32[2,16,3,256]{3,1,2,0:T(8,128)S(1)} copy(f32[2,16,3,256]{2,1,3,0:T(8,128)} %slice.596) | data formatting | bytes 196608 | tf_op jit(solution)/shard_map/slice | solution.py:127
  75.6 4.3 %copy.353 = f32[2,16,16,128,2]{2,4,3,1,0:T(2,128)} copy(f32[2,16,16,128,2]{3,2,1,0,4:T(8,128)S(1)} %pad_maximum_fusion.2) | data formatting | bytes 1048576 | tf_op jit(solution)/shard_map/stack | solution.py:56
  79.9 2.8 %copy.355 = f32[2,8,2,16,256]{4,3,1,0,2:T(8,128)S(1)} copy(f32[2,8,2,16,256]{3,4,2,1,0:T(8,128)} %bitcast.234) | data formatting | bytes 1048576 | tf_op jit(solution)/shard_map/concatenate | solution.py:135
  82.9 0.4 add_bitcast_fusion.1
  84.4 0.4 copy.356
  84.8 9.8 %collective-permute-done.13 = f32[1,8,32,256]{3,1,2,0:T(8,128)S(1)} collective-permute-done((f32[1,8,32,256]{3,1,2,0:T(8,128)S(1)}, f32[1,8,32,256]{3,1,2,0:T(8,128)S(1)}, u32[]{:S(2)}, u32[]{:S(2)}) %collective-permute-start.13) | collective-permute-done | bytes 262176 | tf_op jit(solution)/shard_map/ppermute | solution.py:23
  94.8 6.4 %collective-permute-done.12 = f32[2,8,32,256]{3,1,2,0:T(8,128)S(1)} collective-permute-done((f32[2,8,32,256]{3,1,2,0:T(8,128)S(1)}, f32[2,8,32,256]{3,1,2,0:T(8,128)S(1)}, u32[]{:S(2)}, u32[]{:S(2)}) %collective-permute-start.12) | collective-permute-done | bytes 524320 | tf_op jit(solution)/shard_map/ppermute | solution.py:23
  102.4 0.8 copy.380
  103.3 33.9 %all-reduce = (f32[4]{0:T(128)S(1)}, f32[4]{0:T(128)S(1)}) all-reduce(f32[4]{0:T(128)S(1)} %add.977, f32[4]{0:T(128)S(1)} %get-tuple-element.12), channel_id=1, replica_groups=mesh['cube'=2,'gz'=8,'gy'=2] {'gz','gy'}, use_global_device_ids=true, to_apply=%region_4.5 | all-reduce | flops 8 | bytes 64 | tf_op jit(solution)/shard_map/psum | solution.py:197
  137.2 0.5 multiply_divide_fusion
  (104 shorter events, 7.0 us)
Async XLA Ops:
  0.6 41.6 %copy-start.1 = (f32[4]{0:T(128)S(1)}, f32[4]{0:T(128)}, u32[]{:S(2)}) copy-start(f32[4]{0:T(128)} %param.3) | copy-start | bytes 52
  0.6 11.2 %collective-permute-start = (f32[4,1,32,256]{3,2,0,1:T(8,128)}, f32[4,1,32,256]{3,2,0,1:T(8,128)S(1)}, u32[]{:S(2)}, u32[]{:S(2)}) collective-permute-start(f32[4,1,32,256]{3,2,0,1:T(8,128)} %bitcast.244), channel_id=1, source_target_pairs={{0,14},{2,0},{4,2},{6,4},{8,6},{10,8},{12,10},{14,12},{1,15},{3,1}... | collective-permute-start | bytes 393224 | tf_op jit(solution)/shard_map/ppermute | solution.py:23
  7.6 4.3 %collective-permute-start.1 = (f32[2,1,32,256]{3,2,0,1:T(8,128)S(1)}, f32[2,1,32,256]{3,2,0,1:T(8,128)S(1)}, u32[]{:S(2)}, u32[]{:S(2)}) collective-permute-start(f32[2,1,32,256]{3,2,0,1:T(8,128)S(1)} %slice_bitcast_fusion.4), channel_id=1, source_target_pairs={{0,12},{2,14},{4,0},{6,2},{8,4},{10,6},{12,8},{14,10},{1,13},{3,15... | collective-permute-start | bytes 196616 | tf_op jit(solution)/shard_map/ppermute | solution.py:23
  13.8 1.3 collective-permute-start.2
  34.7 4.7 %collective-permute-start.5 = (f32[2,1,16,128]{3,2,1,0:T(8,128)S(1)}, f32[2,1,16,128]{3,2,1,0:T(8,128)S(1)}, u32[]{:S(2)}, u32[]{:S(2)}) collective-permute-start(f32[2,1,16,128]{3,2,1,0:T(8,128)S(1)} %slice.541), channel_id=1, source_target_pairs={{0,10},{2,12},{4,14},{6,0},{8,2},{10,4},{12,6},{14,8},{1,11},{3,13... | collective-permute-start | bytes 49160 | tf_op jit(solution)/shard_map/ppermute | solution.py:23
  35.7 5.1 %collective-permute-start.4 = (f32[2,1,16,128]{3,2,1,0:T(8,128)S(1)}, f32[2,1,16,128]{3,2,1,0:T(8,128)S(1)}, u32[]{:S(2)}, u32[]{:S(2)}) collective-permute-start(f32[2,1,16,128]{3,2,1,0:T(8,128)S(1)} %slice.541), channel_id=1, source_target_pairs={{0,12},{2,14},{4,0},{6,2},{8,4},{10,6},{12,8},{14,10},{1,13},{3,15... | collective-permute-start | bytes 49160 | tf_op jit(solution)/shard_map/ppermute | solution.py:23
  38.3 3.7 %collective-permute-start.3 = (f32[2,1,16,128]{3,2,1,0:T(8,128)S(1)}, f32[2,1,16,128]{3,2,1,0:T(8,128)S(1)}, u32[]{:S(2)}, u32[]{:S(2)}) collective-permute-start(f32[2,1,16,128]{3,2,1,0:T(8,128)S(1)} %slice.541), channel_id=1, source_target_pairs={{0,14},{2,0},{4,2},{6,4},{8,6},{10,8},{12,10},{14,12},{1,15},{3,1}... | collective-permute-start | bytes 49160 | tf_op jit(solution)/shard_map/ppermute | solution.py:23
  42.1 1.2 collective-permute-start.6
  47.4 1.6 %collective-permute-start.7 = (f32[1,16,3,128]{1,2,3,0:T(4,128)S(1)}, f32[1,16,3,128]{1,2,3,0:T(4,128)S(1)}, u32[]{:S(2)}, u32[]{:S(2)}) collective-permute-start(f32[1,16,3,128]{1,2,3,0:T(4,128)S(1)} %slice.564), channel_id=1, source_target_pairs={{0,1},{1,0},{2,3},{3,2},{4,5},{5,4},{6,7},{7,6},{8,9},{9,8},{10,11... | collective-permute-start | bytes 73736 | tf_op jit(solution)/shard_map/ppermute | solution.py:23
  49.2 7.5 %collective-permute-start.10 = (f32[1,8,16,128]{3,1,2,0:T(8,128)S(1)}, f32[1,8,16,128]{3,1,2,0:T(8,128)S(1)}, u32[]{:S(2)}, u32[]{:S(2)}) collective-permute-start(f32[1,8,16,128]{3,1,2,0:T(8,128)S(1)} %bitcast.270), channel_id=1, source_target_pairs={{0,6},{2,8},{4,10},{6,12},{8,14},{10,0},{12,2},{14,4},{1,7},{3,9},... | collective-permute-start | bytes 196616 | tf_op jit(solution)/shard_map/ppermute | solution.py:23
  53.2 6.1 %collective-permute-start.9 = (f32[1,8,16,128]{3,1,2,0:T(8,128)S(1)}, f32[1,8,16,128]{3,1,2,0:T(8,128)S(1)}, u32[]{:S(2)}, u32[]{:S(2)}) collective-permute-start(f32[1,8,16,128]{3,1,2,0:T(8,128)S(1)} %bitcast.271), channel_id=1, source_target_pairs={{0,4},{2,6},{4,8},{6,10},{8,12},{10,14},{12,0},{14,2},{1,5},{3,7},... | collective-permute-start | bytes 196616 | tf_op jit(solution)/shard_map/ppermute | solution.py:23
  53.2 7.2 %collective-permute-start.8 = (f32[1,8,16,128]{3,1,2,0:T(8,128)S(1)}, f32[1,8,16,128]{3,1,2,0:T(8,128)S(1)}, u32[]{:S(2)}, u32[]{:S(2)}) collective-permute-start(f32[1,8,16,128]{3,1,2,0:T(8,128)S(1)} %bitcast.272), channel_id=1, source_target_pairs={{0,2},{2,4},{4,6},{6,8},{8,10},{10,12},{12,14},{14,0},{1,3},{3,5},... | collective-permute-start | bytes 196616 | tf_op jit(solution)/shard_map/ppermute | solution.py:23
  75.5 7.2 %collective-permute-start.11 = (f32[2,16,3,256]{3,1,2,0:T(8,128)S(1)}, f32[2,16,3,256]{3,1,2,0:T(8,128)S(1)}, u32[]{:S(2)}, u32[]{:S(2)}) collective-permute-start(f32[2,16,3,256]{3,1,2,0:T(8,128)S(1)} %copy.351), channel_id=1, source_target_pairs={{0,1},{1,0},{2,3},{3,2},{4,5},{5,4},{6,7},{7,6},{8,9},{9,8},{10,11... | collective-permute-start | bytes 294920 | tf_op jit(solution)/shard_map/ppermute | solution.py:23
  83.6 17.5 %collective-permute-start.12 = (f32[2,8,32,256]{3,1,2,0:T(8,128)S(1)}, f32[2,8,32,256]{3,1,2,0:T(8,128)S(1)}, u32[]{:S(2)}, u32[]{:S(2)}) collective-permute-start(f32[2,8,32,256]{3,1,2,0:T(8,128)S(1)} %bitcast.258), channel_id=1, source_target_pairs={{0,2},{2,4},{4,6},{6,8},{8,10},{10,12},{12,14},{14,0},{1,3},{3,5},... | collective-permute-start | bytes 1572872 | tf_op jit(solution)/shard_map/ppermute | solution.py:23
  84.1 10.5 %collective-permute-start.13 = (f32[1,8,32,256]{3,1,2,0:T(8,128)S(1)}, f32[1,8,32,256]{3,1,2,0:T(8,128)S(1)}, u32[]{:S(2)}, u32[]{:S(2)}) collective-permute-start(f32[1,8,32,256]{3,1,2,0:T(8,128)S(1)} %bitcast.269), channel_id=1, source_target_pairs={{0,4},{2,6},{4,8},{6,10},{8,12},{10,14},{12,0},{14,2},{1,5},{3,7},... | collective-permute-start | bytes 786440 | tf_op jit(solution)/shard_map/ppermute | solution.py:23
  101.3 0.9 copy-start
where the time goes:
time: 138 us
  local copies, waits for them, and re-layouts  48 us (35%)
  blocking collectives  33.9 us (25%)
  waiting for transfers between devices  32.3 us (23%)
  starting transfers between devices  15.7 us (11%)
  other arithmetic  6.35 us (5%)
  between operations  1.4 us (1%)
    psum x1, blocking collectives, body(): zero_weight = lax.psum(zero_local, ('gz', 'gy'))  33.9 us
    ppermute x14, waiting for transfers between devices, passed_along(): lax.ppermute(array, axis, [(i, (i + by) % devices) for i in range(devices)])  32.3 us
    slice x32, local copies, waits for them, and re-layouts, analyse(): lax.slice_in_dim(extended, tap_index, tap_index + axis_length - 1, 2, dim...  22.2 us
    ppermute x14, starting transfers between devices, passed_along(): lax.ppermute(array, axis, [(i, (i + by) % devices) for i in range(devices)])  15.7 us
    another operation x8, local copies, waits for them, and re-layouts, synthesise(): paired = jnp.stack([even_part, odd_part], dimension_number + 1)  11.1 us
    slice x4, local copies, waits for them, and re-layouts, preceding_panel(): lax.slice_in_dim(input_tensor, axis_length - shift_amount, axis_length, 1...  9.12 us
    concatenate x5, local copies, waits for them, and re-layouts, preceding_panel(): return jnp.concatenate(split_pieces, dimension_number)  3.26 us
  transfers between devices with their start and end apart: 14, of which 12 were waited for; matrix products, arithmetic and copies ran while one was open for 8% of the time, Pallas kernels for 0%

commit v1 on v0

--- a/solution.py
+++ b/solution.py
@@ -194,7 +194,8 @@
         return jnp.sum(square_grid / (square_grid + widened * widened), axis=(1, 2, 3, 4))
 
     zero_local = weights(details_one) + weights(details_two)
-    zero_weight = lax.psum(zero_local, ("gz", "gy"))
+    one_axis = lax.psum(zero_local, "gy")
+    zero_weight = lax.psum(one_axis, "gz")
     count_two = level_two.shape
     coarse_two = jnp.broadcast_to(
         level_two[:, :1], (count_two[0], thresholds.shape[0], count_two[2], count_two[3])

time: 138 us -> 149 us (1.080)
  blocking collectives: 33.9 us -> 60.8 us
  waiting for transfers between devices: 32.3 us -> 16.1 us
    psum x1 -> x3, blocking collectives: 33.9 us -> 60.8 us  [the longest x1 29.5 us: body(): lax.psum(jnp.sum((denoised - noisy_cube[:, None]) ** 2, axis=(0, 2, 3)),...]
    ppermute x14, waiting for transfers between devices: 32.3 us -> 16.1 us  [passed_along(): lax.ppermute(array, axis, [(i, (i + by) % devices) for i in range(devices)])]
  transfers between devices with their start and end apart: 14 -> 14, of which waited for: 12 -> 10; matrix products, arithmetic and copies ran while one was open for 8% -> 7% of each run, Pallas kernels for 0% -> 0%
where the time goes in v1:
time: 149 us; the launch traced here: 148 us
  blocking collectives  60.8 us (41%)
  local copies, waits for them, and re-layouts  48 us (32%)
  waiting for transfers between devices  16.1 us (11%)
  starting transfers between devices  15.7 us (11%)
  other arithmetic  6.34 us (4%)
    psum x1, blocking collectives, body(): lax.psum(jnp.sum((denoised - noisy_cube[:, None]) ** 2, axis=(0, 2, 3)),...  29.5 us
    psum x1, blocking collectives, body(): zero_weight = lax.psum(one_axis, 'gz')  28.7 us
    slice x32, local copies, waits for them, and re-layouts, analyse(): lax.slice_in_dim(extended, tap_index, tap_index + axis_length - 1, 2, dim...  22.2 us
    ppermute x14, waiting for transfers between devices, passed_along(): lax.ppermute(array, axis, [(i, (i + by) % devices) for i in range(devices)])  16.1 us
    ppermute x14, starting transfers between devices, passed_along(): lax.ppermute(array, axis, [(i, (i + by) % devices) for i in range(devices)])  15.7 us
    another operation x8, local copies, waits for them, and re-layouts, synthesise(): paired = jnp.stack([even_part, odd_part], dimension_number + 1)  11.1 us
    slice x4, local copies, waits for them, and re-layouts, preceding_panel(): lax.slice_in_dim(input_tensor, axis_length - shift_amount, axis_length, 1...  9.08 us
    concatenate x5, local copies, waits for them, and re-layouts, preceding_panel(): return jnp.concatenate(split_pieces, dimension_number)  3.26 us
  transfers between devices with their start and end apart: 14, of which 10 were waited for; matrix products, arithmetic and copies ran while one was open for 7% of the time, Pallas kernels for 0%

profile of v1, /device:TPU:0, one launch (start us, length us, event | category | flops | bytes accessed | tf_op | source)
XLA Modules:
  0.0 148.3 jit_solution(10336815150046521559)
XLA Ops:
  0.6 6.1 %collective-permute-start = (f32[4,1,32,256]{3,2,0,1:T(8,128)}, f32[4,1,32,256]{3,2,0,1:T(8,128)S(1)}, u32[]{:S(2)}, u32[]{:S(2)}) collective-permute-start(f32[4,1,32,256]{3,2,0,1:T(8,128)} %bitcast.244), channel_id=1, source_target_pairs={{0,14},{2,0},{4,2},{6,4},{8,6},{10,8},{12,10},{14,12},{1,15},{3,1}... | collective-permute-start | bytes 393224 | tf_op jit(solution)/shard_map/ppermute | solution.py:23
  6.7 0.9 slice_bitcast_fusion.4
  7.6 0.4 collective-permute-start.1
  8.0 3.8 %collective-permute-done.1 = f32[2,1,32,256]{3,2,0,1:T(8,128)S(1)} collective-permute-done((f32[2,1,32,256]{3,2,0,1:T(8,128)S(1)}, f32[2,1,32,256]{3,2,0,1:T(8,128)S(1)}, u32[]{:S(2)}, u32[]{:S(2)}) %collective-permute-start.1) | collective-permute-done | bytes 65568 | tf_op jit(solution)/shard_map/ppermute | solution.py:23
  11.8 0.9 pad_maximum_fusion.5
  12.8 1.0 add_bitcast_fusion.11
  14.0 1.0 collective-permute-done.2
  15.8 2.3 %slice.438 = f32[2,4,16,128]{3,2,1,0:T(8,128)S(1)} slice(f32[2,4,16,256]{3,2,1,0:T(8,128)S(1)} %bitcast.249), slice={[0:2:1], [0:4:1], [0:16:1], [1:256:2]} | slice | bytes 131072 | tf_op jit(solution)/shard_map/slice | solution.py:30
  18.1 2.3 %slice.437 = f32[2,4,16,128]{3,2,1,0:T(8,128)S(1)} slice(f32[2,4,16,256]{3,2,1,0:T(8,128)S(1)} %bitcast.250), slice={[0:2:1], [0:4:1], [0:16:1], [0:255:2]} | slice | bytes 131072 | tf_op jit(solution)/shard_map/slice | solution.py:30
  20.5 2.3 %slice.445 = f32[2,4,16,128]{3,2,1,0:T(8,128)S(1)} slice(f32[2,4,16,262]{3,2,1,0:T(8,128)S(1)} %pad_maximum_fusion.9), slice={[0:2:1], [0:4:1], [0:16:1], [7:262:2]} | slice | bytes 131072 | tf_op jit(solution)/shard_map/slice | solution.py:30
  22.9 2.3 %slice.444 = f32[2,4,16,128]{3,2,1,0:T(8,128)S(1)} slice(f32[2,4,16,262]{3,2,1,0:T(8,128)S(1)} %pad_maximum_fusion.9), slice={[0:2:1], [0:4:1], [0:16:1], [6:261:2]} | slice | bytes 131072 | tf_op jit(solution)/shard_map/slice | solution.py:30
  25.2 2.3 %slice.443 = f32[2,4,16,128]{3,2,1,0:T(8,128)S(1)} slice(f32[2,4,16,262]{3,2,1,0:T(8,128)S(1)} %pad_maximum_fusion.9), slice={[0:2:1], [0:4:1], [0:16:1], [5:260:2]} | slice | bytes 131072 | tf_op jit(solution)/shard_map/slice | solution.py:30
  27.5 2.3 %slice.442 = f32[2,4,16,128]{3,2,1,0:T(8,128)S(1)} slice(f32[2,4,16,262]{3,2,1,0:T(8,128)S(1)} %pad_maximum_fusion.9), slice={[0:2:1], [0:4:1], [0:16:1], [4:259:2]} | slice | bytes 131072 | tf_op jit(solution)/shard_map/slice | solution.py:30
  29.9 2.3 %slice.441 = f32[2,4,16,128]{3,2,1,0:T(8,128)S(1)} slice(f32[2,4,16,262]{3,2,1,0:T(8,128)S(1)} %pad_maximum_fusion.9), slice={[0:2:1], [0:4:1], [0:16:1], [3:258:2]} | slice | bytes 131072 | tf_op jit(solution)/shard_map/slice | solution.py:30
  32.2 2.3 %slice.440 = f32[2,4,16,128]{3,2,1,0:T(8,128)S(1)} slice(f32[2,4,16,262]{3,2,1,0:T(8,128)S(1)} %pad_maximum_fusion.9), slice={[0:2:1], [0:4:1], [0:16:1], [2:257:2]} | slice | bytes 131072 | tf_op jit(solution)/shard_map/slice | solution.py:30
  34.7 0.9 collective-permute-start.5
  35.7 2.7 %collective-permute-start.4 = (f32[2,1,16,128]{3,2,1,0:T(8,128)S(1)}, f32[2,1,16,128]{3,2,1,0:T(8,128)S(1)}, u32[]{:S(2)}, u32[]{:S(2)}) collective-permute-start(f32[2,1,16,128]{3,2,1,0:T(8,128)S(1)} %slice.541), channel_id=1, source_target_pairs={{0,12},{2,14},{4,0},{6,2},{8,4},{10,6},{12,8},{14,10},{1,13},{3,15... | collective-permute-start | bytes 49160 | tf_op jit(solution)/shard_map/ppermute | solution.py:23
  38.6 0.8 collective-permute-done.5
  39.4 1.3 collective-permute-done.4
  40.7 1.3 collective-permute-done.3
  42.2 1.1 collective-permute-done.6
  44.2 0.3 slice.472
  44.5 0.3 slice.471
  44.9 0.3 slice.470
  45.2 0.3 slice.469
  45.5 0.3 slice.468
  45.9 0.3 slice.467
  46.6 0.4 add_bitcast_fusion.5
  47.6 0.6 copy.325
  48.5 0.5 collective-permute-done.7
  49.2 3.8 %collective-permute-start.10 = (f32[1,8,16,128]{3,1,2,0:T(8,128)S(1)}, f32[1,8,16,128]{3,1,2,0:T(8,128)S(1)}, u32[]{:S(2)}, u32[]{:S(2)}) collective-permute-start(f32[1,8,16,128]{3,1,2,0:T(8,128)S(1)} %bitcast.270), channel_id=1, source_target_pairs={{0,6},{2,8},{4,10},{6,12},{8,14},{10,0},{12,2},{14,4},{1,7},{3,9},... | collective-permute-start | bytes 196616 | tf_op jit(solution)/shard_map/ppermute | solution.py:23
  53.2 0.9 collective-permute-start.8
  54.1 2.6 %collective-permute-done.10 = f32[1,8,16,128]{3,1,2,0:T(8,128)S(1)} collective-permute-done((f32[1,8,16,128]{3,1,2,0:T(8,128)S(1)}, f32[1,8,16,128]{3,1,2,0:T(8,128)S(1)}, u32[]{:S(2)}, u32[]{:S(2)}) %collective-permute-start.10) | collective-permute-done | bytes 65568 | tf_op jit(solution)/shard_map/ppermute | solution.py:23
  56.8 2.5 %collective-permute-done.9 = f32[1,8,16,128]{3,1,2,0:T(8,128)S(1)} collective-permute-done((f32[1,8,16,128]{3,1,2,0:T(8,128)S(1)}, f32[1,8,16,128]{3,1,2,0:T(8,128)S(1)}, u32[]{:S(2)}, u32[]{:S(2)}) %collective-permute-start.9) | collective-permute-done | bytes 65568 | tf_op jit(solution)/shard_map/ppermute | solution.py:23
  59.3 1.1 collective-permute-done.8
  60.9 1.3 add_bitcast_fusion.3
  62.3 4.4 %copy.350 = f32[2,16,16,128,2]{2,1,4,3,0:T(8,128)} copy(f32[2,16,16,128,2]{3,2,1,0,4:T(8,128)S(1)} %pad_maximum_fusion.2) | data formatting | bytes 1048576 | tf_op jit(solution)/shard_map/stack | solution.py:56
  66.6 5.3 %slice.596 = f32[2,16,3,256]{2,1,3,0:T(8,128)} slice(f32[2,16,16,256]{2,1,3,0:T(8,128)} %bitcast.235), slice={[0:2], [0:16], [13:16], [0:256]} | slice | bytes 196608 | tf_op jit(solution)/shard_map/slice | solution.py:127
  71.9 3.5 %copy.351 = f32[2,16,3,256]{3,1,2,0:T(8,128)S(1)} copy(f32[2,16,3,256]{2,1,3,0:T(8,128)} %slice.596) | data formatting | bytes 196608 | tf_op jit(solution)/shard_map/slice | solution.py:127
  75.6 4.3 %copy.353 = f32[2,16,16,128,2]{2,4,3,1,0:T(2,128)} copy(f32[2,16,16,128,2]{3,2,1,0,4:T(8,128)S(1)} %pad_maximum_fusion.2) | data formatting | bytes 1048576 | tf_op jit(solution)/shard_map/stack | solution.py:56
  79.9 2.8 %copy.355 = f32[2,8,2,16,256]{4,3,1,0,2:T(8,128)S(1)} copy(f32[2,8,2,16,256]{3,4,2,1,0:T(8,128)} %bitcast.234) | data formatting | bytes 1048576 | tf_op jit(solution)/shard_map/concatenate | solution.py:135
  82.9 0.4 add_bitcast_fusion.1
  84.4 2.6 %psum.22 = f32[4]{0:T(128)S(1)} all-reduce(f32[4]{0:T(128)S(1)} %add.979), channel_id=1, replica_groups=mesh['cube'=2,'gz'=8,'gy'=2] {'gy'}, use_global_device_ids=true, to_apply=%region_4.5 | all-reduce | flops 4 | bytes 32 | tf_op jit(solution)/shard_map/psum | solution.py:197
  87.0 28.7 %psum.23 = f32[4]{0:T(128)S(1)} all-reduce(f32[4]{0:T(128)S(1)} %psum.22), channel_id=1, replica_groups=mesh['cube'=2,'gz'=8,'gy'=2] {'gz'}, use_global_device_ids=true, to_apply=%region_5.6 | all-reduce | flops 4 | bytes 32 | tf_op jit(solution)/shard_map/psum | solution.py:198
  115.7 0.4 copy.356
  117.5 29.5 %psum.21 = f32[4]{0:T(128)S(1)} all-reduce(f32[4]{0:T(128)S(1)} %get-tuple-element.10), channel_id=1, replica_groups=mesh['cube'=2,'gz'=8,'gy'=2] {'gz','gy'}, use_global_device_ids=true, to_apply=%region_1.0 | all-reduce | flops 4 | bytes 32 | tf_op jit(solution)/shard_map/psum | solution.py:205
  147.0 0.8 copy.380
  147.8 0.5 multiply_divide_fusion
  (106 shorter events, 7.0 us)
Async XLA Ops:
  0.6 41.6 %copy-start.1 = (f32[4]{0:T(128)S(1)}, f32[4]{0:T(128)}, u32[]{:S(2)}) copy-start(f32[4]{0:T(128)} %param.3) | copy-start | bytes 52
  0.6 11.2 %collective-permute-start = (f32[4,1,32,256]{3,2,0,1:T(8,128)}, f32[4,1,32,256]{3,2,0,1:T(8,128)S(1)}, u32[]{:S(2)}, u32[]{:S(2)}) collective-permute-start(f32[4,1,32,256]{3,2,0,1:T(8,128)} %bitcast.244), channel_id=1, source_target_pairs={{0,14},{2,0},{4,2},{6,4},{8,6},{10,8},{12,10},{14,12},{1,15},{3,1}... | collective-permute-start | bytes 393224 | tf_op jit(solution)/shard_map/ppermute | solution.py:23
  7.6 4.3 %collective-permute-start.1 = (f32[2,1,32,256]{3,2,0,1:T(8,128)S(1)}, f32[2,1,32,256]{3,2,0,1:T(8,128)S(1)}, u32[]{:S(2)}, u32[]{:S(2)}) collective-permute-start(f32[2,1,32,256]{3,2,0,1:T(8,128)S(1)} %slice_bitcast_fusion.4), channel_id=1, source_target_pairs={{0,12},{2,14},{4,0},{6,2},{8,4},{10,6},{12,8},{14,10},{1,13},{3,15... | collective-permute-start | bytes 196616 | tf_op jit(solution)/shard_map/ppermute | solution.py:23
  13.8 1.3 collective-permute-start.2
  34.7 4.7 %collective-permute-start.5 = (f32[2,1,16,128]{3,2,1,0:T(8,128)S(1)}, f32[2,1,16,128]{3,2,1,0:T(8,128)S(1)}, u32[]{:S(2)}, u32[]{:S(2)}) collective-permute-start(f32[2,1,16,128]{3,2,1,0:T(8,128)S(1)} %slice.541), channel_id=1, source_target_pairs={{0,10},{2,12},{4,14},{6,0},{8,2},{10,4},{12,6},{14,8},{1,11},{3,13... | collective-permute-start | bytes 49160 | tf_op jit(solution)/shard_map/ppermute | solution.py:23
  35.7 5.1 %collective-permute-start.4 = (f32[2,1,16,128]{3,2,1,0:T(8,128)S(1)}, f32[2,1,16,128]{3,2,1,0:T(8,128)S(1)}, u32[]{:S(2)}, u32[]{:S(2)}) collective-permute-start(f32[2,1,16,128]{3,2,1,0:T(8,128)S(1)} %slice.541), channel_id=1, source_target_pairs={{0,12},{2,14},{4,0},{6,2},{8,4},{10,6},{12,8},{14,10},{1,13},{3,15... | collective-permute-start | bytes 49160 | tf_op jit(solution)/shard_map/ppermute | solution.py:23
  38.3 3.7 %collective-permute-start.3 = (f32[2,1,16,128]{3,2,1,0:T(8,128)S(1)}, f32[2,1,16,128]{3,2,1,0:T(8,128)S(1)}, u32[]{:S(2)}, u32[]{:S(2)}) collective-permute-start(f32[2,1,16,128]{3,2,1,0:T(8,128)S(1)} %slice.541), channel_id=1, source_target_pairs={{0,14},{2,0},{4,2},{6,4},{8,6},{10,8},{12,10},{14,12},{1,15},{3,1}... | collective-permute-start | bytes 49160 | tf_op jit(solution)/shard_map/ppermute | solution.py:23
  42.1 1.2 collective-permute-start.6
  47.4 1.6 %collective-permute-start.7 = (f32[1,16,3,128]{1,2,3,0:T(4,128)S(1)}, f32[1,16,3,128]{1,2,3,0:T(4,128)S(1)}, u32[]{:S(2)}, u32[]{:S(2)}) collective-permute-start(f32[1,16,3,128]{1,2,3,0:T(4,128)S(1)} %slice.564), channel_id=1, source_target_pairs={{0,1},{1,0},{2,3},{3,2},{4,5},{5,4},{6,7},{7,6},{8,9},{9,8},{10,11... | collective-permute-start | bytes 73736 | tf_op jit(solution)/shard_map/ppermute | solution.py:23
  49.2 7.5 %collective-permute-start.10 = (f32[1,8,16,128]{3,1,2,0:T(8,128)S(1)}, f32[1,8,16,128]{3,1,2,0:T(8,128)S(1)}, u32[]{:S(2)}, u32[]{:S(2)}) collective-permute-start(f32[1,8,16,128]{3,1,2,0:T(8,128)S(1)} %bitcast.270), channel_id=1, source_target_pairs={{0,6},{2,8},{4,10},{6,12},{8,14},{10,0},{12,2},{14,4},{1,7},{3,9},... | collective-permute-start | bytes 196616 | tf_op jit(solution)/shard_map/ppermute | solution.py:23
  53.2 6.1 %collective-permute-start.9 = (f32[1,8,16,128]{3,1,2,0:T(8,128)S(1)}, f32[1,8,16,128]{3,1,2,0:T(8,128)S(1)}, u32[]{:S(2)}, u32[]{:S(2)}) collective-permute-start(f32[1,8,16,128]{3,1,2,0:T(8,128)S(1)} %bitcast.271), channel_id=1, source_target_pairs={{0,4},{2,6},{4,8},{6,10},{8,12},{10,14},{12,0},{14,2},{1,5},{3,7},... | collective-permute-start | bytes 196616 | tf_op jit(solution)/shard_map/ppermute | solution.py:23
  53.2 7.2 %collective-permute-start.8 = (f32[1,8,16,128]{3,1,2,0:T(8,128)S(1)}, f32[1,8,16,128]{3,1,2,0:T(8,128)S(1)}, u32[]{:S(2)}, u32[]{:S(2)}) collective-permute-start(f32[1,8,16,128]{3,1,2,0:T(8,128)S(1)} %bitcast.272), channel_id=1, source_target_pairs={{0,2},{2,4},{4,6},{6,8},{8,10},{10,12},{12,14},{14,0},{1,3},{3,5},... | collective-permute-start | bytes 196616 | tf_op jit(solution)/shard_map/ppermute | solution.py:23
  75.5 7.2 %collective-permute-start.11 = (f32[2,16,3,256]{3,1,2,0:T(8,128)S(1)}, f32[2,16,3,256]{3,1,2,0:T(8,128)S(1)}, u32[]{:S(2)}, u32[]{:S(2)}) collective-permute-start(f32[2,16,3,256]{3,1,2,0:T(8,128)S(1)} %copy.351), channel_id=1, source_target_pairs={{0,1},{1,0},{2,3},{3,2},{4,5},{5,4},{6,7},{7,6},{8,9},{9,8},{10,11... | collective-permute-start | bytes 294920 | tf_op jit(solution)/shard_map/ppermute | solution.py:23
  83.6 32.6 %collective-permute-start.12 = (f32[2,8,32,256]{3,1,2,0:T(8,128)S(1)}, f32[2,8,32,256]{3,1,2,0:T(8,128)S(1)}, u32[]{:S(2)}, u32[]{:S(2)}) collective-permute-start(f32[2,8,32,256]{3,1,2,0:T(8,128)S(1)} %bitcast.258), channel_id=1, source_target_pairs={{0,2},{2,4},{4,6},{6,8},{8,10},{10,12},{12,14},{14,0},{1,3},{3,5},... | collective-permute-start | bytes 1572872 | tf_op jit(solution)/shard_map/ppermute | solution.py:23
  84.1 32.0 %collective-permute-start.13 = (f32[1,8,32,256]{3,1,2,0:T(8,128)S(1)}, f32[1,8,32,256]{3,1,2,0:T(8,128)S(1)}, u32[]{:S(2)}, u32[]{:S(2)}) collective-permute-start(f32[1,8,32,256]{3,1,2,0:T(8,128)S(1)} %bitcast.269), channel_id=1, source_target_pairs={{0,4},{2,6},{4,8},{6,10},{8,12},{10,14},{12,0},{14,2},{1,5},{3,7},... | collective-permute-start | bytes 786440 | tf_op jit(solution)/shard_map/ppermute | solution.py:23
  116.4 0.9 copy-start
